TPU v7x, 32 devices: a whole 2x2x4 slice. The times are simulated.
32 devices in a mesh: grp: 4 (over z), slab: 8 (over y, x, core).
Axes of the slice: x: 2, y: 2, z: 4, core: 2. Of those that a mesh axis runs over, the one named last changes fastest.
Arguments:
- orbitals: float32 [8, 96, 9216], P('grp', 'slab'), may hold values from -6 to 6
- occupation: int32 [8], P('grp'), may hold values from 1 to 4
- kernel_hat: float32 [192, 36864], P('slab'), may hold values from 0.02 to 1200, as said below
- pair_mask: int32 [1], replicated, may hold values from 1 to 3
Outputs:
- exchange_terms: float32 [8, 96, 9216], P('grp', 'slab')
Inputs may be any that keep to these rules, and one draw needn't show every extreme that they name: In this round group g is paired with group g XOR pair_mask. kernel_hat is positive, and unchanged when each frequency index k is replaced by (192 - k) mod 192 in all three dimensions at once.
All inputs are finite; a program needn't handle non-finite values.
Results may differ from a plain program's by a relative error of at most 0.0001.
Values sent between devices are 32-bit elements; how exact they have to be, the bound alone decides.
A program may use at most 64 MiB of HBM per device.

v0:
```python
import math

import jax
import jax.numpy as jnp
import ml_dtypes
import numpy as np
from jax import lax
from jax.experimental import pallas as pl
from jax.experimental.pallas import tpu as pltpu
from jax.sharding import PartitionSpec as P

LANE = 128


def halves(table):
    high = table.astype(np.float32).astype(ml_dtypes.bfloat16)
    low = (table - high.astype(np.float64)).astype(ml_dtypes.bfloat16)
    return np.stack([high, low])


class Plan:
    def __init__(self, planes, plane_cells, slabs, freqs):
        self.planes = planes
        self.grid = math.isqrt(plane_cells)
        self.slabs = slabs
        self.freqs = freqs
        self.period = 2 * self.grid
        self.group = math.lcm(self.grid, LANE)
        self.fold = self.group // self.grid
        self.chunks = self.grid // self.fold
        self.rows = planes * self.chunks
        self.groups = -(-planes // self.fold)
        self.lanes = self.groups * self.group
        self.wide = 2 * LANE
        self.starts = []
        for fold in range(self.fold):
            start = fold * self.grid // LANE * LANE
            self.starts.append(min(start, self.group - self.wide))
        self.spectrum = 2 * self.period
        self.padded = -(-self.period // self.wide) * self.wide

    def wave(self, left, right):
        angle = 2.0 * math.pi / self.period * (np.outer(left, right) % self.period)
        return np.cos(angle), np.sin(angle)

    def tables(self):
        grid, period, fold = self.grid, self.period, self.fold
        cells = np.arange(grid)
        waves = np.arange(period)
        cos, sin = self.wave(cells, waves)
        cosi, sini = cos.T / period, sin.T / period
        column = [
            (part, owner * self.freqs + own)
            for owner in range(self.slabs)
            for part in range(2)
            for own in range(self.freqs)
        ]
        part = np.array([c[0] for c in column])
        freq = np.array([c[1] for c in column])
        zf = np.zeros((fold, 2, self.wide, self.spectrum))
        zi = np.zeros((fold, self.spectrum, 2, self.wide))
        yf = np.zeros((fold, self.wide, 2, self.padded))
        yi = np.zeros((fold, self.padded, 2, self.wide))
        y_order = np.array([fold * q + j for j in range(fold) for q in range(self.chunks)])
        for j in range(fold):
            at = slice(j * grid - self.starts[j], (j + 1) * grid - self.starts[j])
            zf[j, 0, at] = np.where(part == 0, cos[:, freq], -sin[:, freq])
            zf[j, 1, at] = np.where(part == 0, sin[:, freq], cos[:, freq])
            zi[j, :, 0, at] = np.where(part == 0, cosi[freq].T, -sini[freq].T).T
            zi[j, :, 1, at] = np.where(part == 0, sini[freq].T, cosi[freq].T).T
            yf[j, at, 0, :period] = cos[y_order]
            yf[j, at, 1, :period] = sin[y_order]
            yi[j, :period, 0, at] = cosi[:, y_order]
            yi[j, :period, 1, at] = sini[:, y_order]
        row = [
            (c, s * self.planes + x)
            for x in range(self.planes)
            for s in range(self.slabs)
            for c in range(2)
        ]
        side = np.array([r[0] for r in row])
        cell = np.array([r[1] for r in row])
        xf = np.concatenate(
            [
                np.where(side == 0, cos[cell].T, sin[cell].T),
                np.where(side == 0, -sin[cell].T, cos[cell].T),
            ]
        )
        xi = np.concatenate(
            [
                np.where(side == 0, cosi[:, cell], sini[:, cell]),
                np.where(side == 0, -sini[:, cell], cosi[:, cell]),
            ]
        ).T
        return {
            "zf": halves(zf),
            "zi": halves(zi.reshape(fold, self.spectrum, 2 * self.wide)),
            "yf": halves(yf.reshape(fold, self.wide, 2 * self.padded)),
            "yi": halves(yi.reshape(fold, self.padded, 2 * self.wide)),
            "xf": halves(xf),
            "xi": halves(xi),
        }


def mm(left, right):
    return jnp.dot(left, right, preferred_element_type=jnp.float32)


def split(value):
    high = value.astype(jnp.bfloat16)
    low = (value - high.astype(jnp.float32)).astype(jnp.bfloat16)
    return high, low


def right_mul(value, high, low):
    vh, vl = value
    return mm(vh, high) + mm(vh, low) + mm(vl, high)


def left_mul(high, low, value):
    vh, vl = value
    return mm(high, vh) + mm(low, vh) + mm(high, vl)


def forward_z(plan, left_ref, right_ref, table_ref, out_ref, turned):
    right = right_ref[...]
    densities = [split(left_ref[i] * right) for i in range(2)]
    used = plan.planes * plan.grid
    if used < plan.lanes:
        turned[used:, :] = jnp.zeros((plan.lanes - used, plan.spectrum), jnp.float32)
    chunks, grid, wide = plan.chunks, plan.grid, plan.wide
    for j in range(plan.fold):
        at = slice(plan.starts[j], plan.starts[j] + wide)
        total = None
        for i in range(2):
            piece = tuple(d[:, at] for d in densities[i])
            term = right_mul(piece, table_ref[0, j, i], table_ref[1, j, i])
            total = term if total is None else total + term
        for x in range(plan.planes):
            first = x * grid + j * chunks
            turned[first : first + chunks, :] = total[x * chunks : (x + 1) * chunks]
    for r in range(turned.shape[0] // LANE):
        for c in range(turned.shape[1] // LANE):
            block = turned[r * LANE : (r + 1) * LANE, c * LANE : (c + 1) * LANE]
            out_ref[c * LANE : (c + 1) * LANE, r * LANE : (r + 1) * LANE] = block.T


def plane_work(plan, spread_ref, kernel_ref, yf_ref, yi_ref, xf_ref, xi_ref, out_ref, *lines):
    slabs, freqs, fold, wide = plan.slabs, plan.freqs, plan.fold, plan.wide
    padded, spectrum = plan.padded, plan.spectrum
    tiles = len(lines)
    for x in range(plan.planes):
        g, j = divmod(x, fold)
        start = g * plan.group + plan.starts[j]
        piece = split(spread_ref[:, start : start + wide])
        both = right_mul(piece, yf_ref[0, j], yf_ref[1, j])
        both = both.reshape(slabs, 2, freqs, 2 * padded)
        real = both[:, 0, :, :padded] + both[:, 1, :, padded:]
        imag = both[:, 1, :, :padded] - both[:, 0, :, padded:]
        mixed = jnp.stack([real, imag], axis=1).reshape(spectrum, padded)
        for t in range(tiles):
            lines[t][x * spectrum : (x + 1) * spectrum, :] = mixed[:, t * LANE : (t + 1) * LANE]

    def one_plane(k, carry):
        rows = pl.ds(k, plan.planes * slabs * 2, stride=freqs)
        field = jnp.concatenate([lines[t][rows, :] for t in range(tiles)], axis=1)
        spectra = left_mul(xf_ref[0], xf_ref[1], split(field))
        kernel = kernel_ref[k]
        spectra = jnp.concatenate(
            [spectra[: plan.period] * kernel, spectra[plan.period :] * kernel], axis=0
        )
        back = left_mul(xi_ref[0], xi_ref[1], split(spectra))
        for t in range(tiles):
            lines[t][rows, :] = back[:, t * LANE : (t + 1) * LANE]
        return carry

    lax.fori_loop(0, freqs, one_plane, 0)

    for g in range(plan.groups):
        total = [None] * (plan.group // LANE)
        for j in range(fold):
            x = g * fold + j
            if x >= plan.planes:
                break
            rows = slice(x * spectrum, (x + 1) * spectrum)
            field = jnp.concatenate([lines[t][rows, :] for t in range(tiles)], axis=1)
            both = right_mul(split(field), yi_ref[0, j], yi_ref[1, j])
            both = both.reshape(slabs, 2, freqs, 2 * wide)
            real = both[:, 0, :, :wide] - both[:, 1, :, wide:]
            imag = both[:, 1, :, :wide] + both[:, 0, :, wide:]
            mixed = jnp.stack([real, imag], axis=1).reshape(spectrum, wide)
            for t in range(wide // LANE):
                spot = plan.starts[j] // LANE + t
                term = mixed[:, t * LANE : (t + 1) * LANE]
                total[spot] = term if total[spot] is None else total[spot] + term
        for t, term in enumerate(total):
            if term is None:
                term = jnp.zeros((spectrum, LANE), jnp.float32)
            first = g * plan.group + t * LANE
            out_ref[:, first : first + LANE] = term


def inverse_z(plan, spread_ref, left_ref, right_ref, table_ref, near_ref, far_ref, turned):
    chunks, grid, wide = plan.chunks, plan.grid, plan.wide
    for r in range(turned.shape[0] // LANE):
        for c in range(turned.shape[1] // LANE):
            block = spread_ref[c * LANE : (c + 1) * LANE, r * LANE : (r + 1) * LANE]
            turned[r * LANE : (r + 1) * LANE, c * LANE : (c + 1) * LANE] = block.T
    total = [[None] * (plan.group // LANE) for _ in range(2)]
    for j in range(plan.fold):
        firsts = [x * grid + j * chunks for x in range(plan.planes)]
        rows = jnp.concatenate([turned[f : f + chunks, :] for f in firsts], axis=0)
        both = right_mul(split(rows), table_ref[0, j], table_ref[1, j])
        for i in range(2):
            for t in range(wide // LANE):
                spot = plan.starts[j] // LANE + t
                first = i * wide + t * LANE
                term = both[:, first : first + LANE]
                known = total[i][spot]
                total[i][spot] = term if known is None else known + term
    right = right_ref[...]
    far = None
    for i in range(2):
        field = jnp.concatenate(total[i], axis=1)
        near_ref[i] = field * right
        term = field * left_ref[i]
        far = term if far is None else far + term
    far_ref[...] = far


def call(body, outs, scratch, *operands):
    return pl.pallas_call(
        body,
        out_shape=outs,
        in_specs=[pl.BlockSpec(memory_space=pltpu.VMEM)] * len(operands),
        out_specs=jax.tree.map(lambda _: pl.BlockSpec(memory_space=pltpu.VMEM), outs),
        scratch_shapes=scratch,
        compiler_params=pltpu.CompilerParams(vmem_limit_bytes=60 * 2**20),
    )(*operands)


def is_wide(group, mask):
    lower = jnp.minimum(group, group ^ mask)
    return (group == lower) == (lower % 2 == 0)


def local(orbitals, occupation, kernel_hat, pair_mask):
    orbit_count, planes, plane_cells = orbitals.shape
    assert orbit_count == 2
    slabs = lax.axis_size("slab")
    groups = lax.axis_size("grp")
    plan = Plan(planes, plane_cells, slabs, kernel_hat.shape[0])
    tables = {name: jnp.asarray(t) for name, t in plan.tables().items()}
    f32 = jnp.float32
    flat = jax.ShapeDtypeStruct((plan.rows, plan.group), f32)
    twin = jax.ShapeDtypeStruct((2, plan.rows, plan.group), f32)
    spread = jax.ShapeDtypeStruct((plan.spectrum, plan.lanes), f32)
    turned = pltpu.VMEM((plan.lanes, plan.spectrum), f32)

    own_group = lax.axis_index("grp")
    partner_bits = pair_mask[0]
    wide_side = is_wide(own_group, partner_bits)
    scale = jnp.sqrt(0.25 * occupation.astype(f32))[:, None, None]
    own = (orbitals * scale).reshape(2, plan.rows, plan.group)

    def pairs(mask, wanted):
        chosen = []
        for g in range(groups):
            lower = min(g, g ^ mask)
            wide = (g == lower) == (lower % 2 == 0)
            if wanted is None or wide == wanted:
                chosen.append((g, g ^ mask))
        return chosen

    def exchange(mask):
        def run(own, kernel_hat):
            first = lax.ppermute(own[0], "grp", pairs(mask, None))
            second = lax.ppermute(own[1], "grp", pairs(mask, True))
            cube = kernel_hat.reshape(-1, plan.period, plan.period)
            cube = jnp.swapaxes(cube, 1, 2)
            cube = jnp.pad(cube, ((0, 0), (0, 0), (0, plan.padded - plan.period)))
            return first, second, cube

        return run

    def give_back(mask):
        def run(both, second):
            return (
                lax.ppermute(both, "grp", pairs(mask, None)),
                lax.ppermute(second, "grp", pairs(mask, False)),
            )

        return run

    masks = range(1, groups)
    index = partner_bits - 1
    first, second, cube = lax.switch(index, [exchange(m) for m in masks], own, kernel_hat)
    left = jnp.where(wide_side, own, jnp.stack([first, second]))
    right = jnp.where(wide_side, first, own[1])
    sent = call(
        lambda *refs: forward_z(plan, *refs), spread, [turned], left, right, tables["zf"]
    )
    here = lax.all_to_all(sent, "slab", split_axis=0, concat_axis=0, tiled=True)
    lines = [
        pltpu.VMEM((planes * plan.spectrum, LANE), f32) for _ in range(plan.padded // LANE)
    ]
    done = call(
        lambda *refs: plane_work(plan, *refs),
        spread,
        lines,
        here,
        cube,
        tables["yf"],
        tables["yi"],
        tables["xf"],
        tables["xi"],
    )
    back = lax.all_to_all(done, "slab", split_axis=0, concat_axis=0, tiled=True)
    near, far = call(
        lambda *refs: inverse_z(plan, *refs),
        (twin, flat),
        [turned],
        back,
        left,
        right,
        tables["zi"],
    )
    back_first, back_second = lax.switch(
        index, [give_back(m) for m in masks], jnp.where(wide_side, far, near[0]), near[1]
    )
    row_first = back_first + jnp.where(wide_side, near[0], 0.0)
    row_second = jnp.where(wide_side, near[1] + back_second, far)
    total = jnp.stack([row_first, row_second]).reshape(orbitals.shape)
    return total * (-1.0 / scale)


def solution(mesh):
    return jax.shard_map(
        local,
        mesh=mesh,
        in_specs=(P("grp", "slab", None), P("grp"), P("slab", None), P()),
        out_specs=P("grp", "slab", None),
        check_vma=False,
    )
```

profile of v0, /device:TPU:16, one launch (start us, length us, event | category | flops | bytes accessed | tf_op | source)
XLA Modules:
  0.0 185.8 jit_solution(12721841745998037453)
XLA Ops:
  2.9 2.1 %slice_reduce_fusion = f32[12,9216]{1,0:T(8,128)} fusion(f32[2,12,9216]{2,0,1:T(2,128)S(1)} %broadcast_multiply_fusion), kind=kLoop, calls=%fused_computation.9 | loop fusion | bytes 884736 | tf_op jit(solution)/shard_map/slice | solution.py:299
  6.3 1.9 %squeeze.33 = f32[288,384]{1,0:T(8,128)} reshape(f32[12,9216]{1,0:T(8,128)} %slice_reduce_fusion) | data formatting | bytes 884736 | tf_op jit(solution)/shard_map/squeeze | solution.py:299
  8.2 2.3 %reshape.26 = f32[2,288,384]{2,1,0:T(8,128)} reshape(f32[2,12,9216]{2,1,0:T(8,128)} %copy.15) | data formatting | bytes 1769472 | tf_op jit(solution)/shard_map/reshape | solution.py:264
  10.5 32.9 %conditional.2 = (f32[288,384]{1,0:T(8,128)}, f32[1,288,384]{2,1,0:T(8,128)}, f32[1,288,384]{2,1,0:T(8,128)}, f32[24,192,256]{2,1,0:T(8,128)}) conditional(s32[]{:T(128)} %clamp.4, (f32[2,288,384]{2,1,0:T(8,128)}, f32[24,36864]{1,0:T(8,128)S(1)}) %tuple.51, (f32[2,288,384]{2,1,0:T(8,128)}, f32[24,36864]{1,0:T(8,128)S(1)}) %tuple.52, ...), branch_computations={%region_0.1_spmd, %region_1.2_spmd, %region_2.3_spmd} | conditional | bytes 28606580 | solution.py:297
  10.5 2.1 %slice_bitcast_fusion.2 = (f32[288,384]{1,0:T(8,128)}, f32[288,384]{1,0:T(8,128)}) fusion(f32[2,288,384]{2,1,0:T(8,128)} %get-tuple-element.33), kind=kLoop, calls=%fused_computation.2 | loop fusion | bytes 1769472 | tf_op jit(solution)/shard_map/cond/branch_1_fun/squeeze | solution.py:278
  13.9 3.8 %reshape.23 = f32[24,192,192]{2,1,0:T(8,128)} reshape(f32[24,36864]{1,0:T(8,128)S(1)} %get-tuple-element.34) | data formatting | bytes 7077888 | tf_op jit(solution)/shard_map/cond/branch_1_fun/reshape | solution.py:279
  17.7 6.4 %copy.22 = f32[24,192,192]{2,1,0:T(8,128)} copy(f32[24,192,192]{1,2,0:T(8,128)} %bitcast.38) | data formatting | bytes 7077888 | tf_op jit(solution)/shard_map/cond
  24.1 4.9 %pad.8.clone = f32[24,192,256]{2,1,0:T(8,128)} pad(f32[24,192,192]{2,1,0:T(8,128)} %copy.22, f32[]{:T(128)} %constant.39.clone), padding=0_0x0_0x0_64 | pad | bytes 8257540 | tf_op jit(solution)/shard_map/cond/branch_1_fun/jit(_pad)/pad | solution.py:281
  29.0 12.6 %collective-permute-done.8 = f32[288,384]{1,0:T(8,128)} collective-permute-done((f32[288,384]{1,0:T(8,128)}, f32[288,384]{1,0:T(8,128)}, u32[]{:S(2)}, u32[]{:S(2)}) %collective-permute-start.8) | collective-permute-done | bytes 442400 | tf_op jit(solution)/shard_map/cond/branch_1_fun/ppermute | solution.py:277
  41.6 1.8 copy.29
  43.5 1.9 broadcast_select_fusion.refs_1_.refs_2_
  45.3 2.1 %maximum_select_fusion.refs_0_.refs_1_ = f32[2,288,384]{2,1,0:T(8,128)} fusion(f32[2,288,384]{2,1,0:T(8,128)} %reshape.26, f32[1,288,384]{2,1,0:T(8,128)} %get-tuple-element.52, f32[1,288,384]{2,1,0:T(8,128)} %get-tuple-element.51, pred[]{:T(512)S(6)} %eq.13), kind=kLoop, calls=%fused_computation.7 | loop fusion | flops 442368 | bytes 2654209 | tf_op jit(solution)/shard_map/jit(_where)/select_n | solution.py:298
  47.4 6.0 %shard_map.100 = f32[384,1152]{1,0:T(8,128)} custom-call(f32[2,288,384]{2,1,0:T(8,128)} %maximum_select_fusion.refs_0_.refs_1_, f32[288,384]{1,0:T(8,128)} %broadcast_select_fusion.refs_1_.refs_2_, bf16[2,4,2,256,384]{4,3,2,1,0:T(8,128)(2,1)} %constant.49.clone.refs_2_), custom_call_target="tpu_custom_call" | custom-call | tf_op jit(solution)/shard_map/pallas_call | solution.py:232
  53.4 27.4 %all_to_all.22 = f32[8,48,1152]{2,1,0:T(8,128)} all-to-all(f32[8,48,1152]{2,1,0:T(8,128)} %bitcast.43), channel_id=1, replica_groups=mesh['grp'=4,'slab'=8] {'slab'}, dimensions={0} | all-to-all | bytes 3538944 | tf_op jit(solution)/shard_map/all_to_all | solution.py:303
  80.8 33.7 %shard_map.101 = f32[384,1152]{1,0:T(8,128)} custom-call(f32[384,1152]{1,0:T(8,128)} %bitcast.40, f32[24,192,256]{2,1,0:T(8,128)} %get-tuple-element.59.refs_1_, bf16[2,4,256,512]{3,2,1,0:T(8,128)(2,1)} %constant.51.clone.refs_2_, bf16[2,4,256,512]{3,2,1,0:T(8,128)(2,1)} %constant.52.clone.refs_3_, bf16[2,384,192]{2,1,0:T(8,128)(2,1)} %constant.53.clone.refs_4_, ...), custom_call_target="tpu_custom_call" | custom-call | tf_op jit(solution)/shard_map/pallas_call | solution.py:232
  114.5 27.4 %all_to_all.23 = f32[8,48,1152]{2,1,0:T(8,128)} all-to-all(f32[8,48,1152]{2,1,0:T(8,128)} %bitcast.41), channel_id=1, replica_groups=mesh['grp'=4,'slab'=8] {'slab'}, dimensions={0} | all-to-all | bytes 3538944 | tf_op jit(solution)/shard_map/all_to_all | solution.py:318
  141.8 6.3 %shard_map.102 = (f32[2,288,384]{2,1,0:T(8,128)}, f32[288,384]{1,0:T(8,128)}) custom-call(f32[384,1152]{1,0:T(8,128)} %bitcast.42, f32[2,288,384]{2,1,0:T(8,128)} %maximum_select_fusion.refs_0_.refs_1_, f32[288,384]{1,0:T(8,128)} %broadcast_select_fusion.refs_1_.refs_2_, bf16[2,4,384,512]{3,2,1,0:T(8,128)(2,1)} %constant.50.clone.refs_3_), custom_call_target="tpu_custom_call" | custom-call | tf_op jit(solution)/shard_map/pallas_call | solution.py:232
  150.3 32.0 %conditional.3 = (f32[288,384]{1,0:T(8,128)}, f32[288,384]{1,0:T(8,128)}) conditional(s32[]{:T(128)} %clamp.4, (f32[288,384]{1,0:T(8,128)S(1)}, f32[288,384]{1,0:T(8,128)S(1)}) %tuple.36, (f32[288,384]{1,0:T(8,128)S(1)}, f32[288,384]{1,0:T(8,128)S(1)}) %tuple.36, (f32[288,384]{1,0:T(8,128)S(1)}, f32[288,384]{1,0:T(8,128)S(1)}) %tuple.36), branch_computations={%region_3.4_spmd, %region_4.5_spmd, %region_5.6_spmd} | conditional | bytes 3539040 | solution.py:328
  150.3 3.8 %collective-permute-start.2 = (f32[288,384]{1,0:T(8,128)S(1)}, f32[288,384]{1,0:T(8,128)}, u32[]{:S(2)}, u32[]{:S(2)}) collective-permute-start(f32[288,384]{1,0:T(8,128)S(1)} %get-tuple-element.39), channel_id=1, source_target_pairs={{0,16},{8,24},{16,0},{24,8},{1,17},{9,25},{17,1},{25,9},{2,18},{10... | collective-permute-start | bytes 1327112 | tf_op jit(solution)/shard_map/cond/branch_1_fun/ppermute | solution.py:289
  154.1 2.7 %collective-permute-start.3 = (f32[288,384]{1,0:T(8,128)S(1)}, f32[288,384]{1,0:T(8,128)}, u32[]{:S(2)}, u32[]{:S(2)}) collective-permute-start(f32[288,384]{1,0:T(8,128)S(1)} %get-tuple-element.40), channel_id=1, source_target_pairs={{8,24},{16,0},{9,25},{17,1},{10,26},{18,2},{11,27},{19,3},{12,28},... | collective-permute-start | bytes 1327112 | tf_op jit(solution)/shard_map/cond/branch_1_fun/ppermute | solution.py:290
  156.8 16.9 %collective-permute-done.2 = f32[288,384]{1,0:T(8,128)} collective-permute-done((f32[288,384]{1,0:T(8,128)S(1)}, f32[288,384]{1,0:T(8,128)}, u32[]{:S(2)}, u32[]{:S(2)}) %collective-permute-start.2) | collective-permute-done | bytes 442400 | tf_op jit(solution)/shard_map/cond/branch_1_fun/ppermute | solution.py:289
  173.7 8.5 %collective-permute-done.3 = f32[288,384]{1,0:T(8,128)} collective-permute-done((f32[288,384]{1,0:T(8,128)S(1)}, f32[288,384]{1,0:T(8,128)}, u32[]{:S(2)}, u32[]{:S(2)}) %collective-permute-start.3) | collective-permute-done | bytes 442400 | tf_op jit(solution)/shard_map/cond/branch_1_fun/ppermute | solution.py:290
  182.2 1.7 fusion
  184.2 1.6 copy.17
  (13 shorter events, 7.2 us)
Async XLA Ops:
  2.9 7.6 %copy-start = (f32[24,36864]{1,0:T(8,128)S(1)}, f32[24,36864]{1,0:T(8,128)}, u32[]{:S(2)}) copy-start(f32[24,36864]{1,0:T(8,128)} %param.18) | copy-start | bytes 10616836
  12.6 29.0 %collective-permute-start.8 = (f32[288,384]{1,0:T(8,128)}, f32[288,384]{1,0:T(8,128)}, u32[]{:S(2)}, u32[]{:S(2)}) collective-permute-start(f32[288,384]{1,0:T(8,128)} %get-tuple-element.63), channel_id=1, source_target_pairs={{0,16},{8,24},{16,0},{24,8},{1,17},{9,25},{17,1},{25,9},{2,18},{10... | collective-permute-start | bytes 1327112 | tf_op jit(solution)/shard_map/cond/branch_1_fun/ppermute | solution.py:277
  12.6 30.8 %collective-permute-start.9 = (f32[288,384]{1,0:T(8,128)}, f32[288,384]{1,0:T(8,128)}, u32[]{:S(2)}, u32[]{:S(2)}) collective-permute-start(f32[288,384]{1,0:T(8,128)} %get-tuple-element.62), channel_id=1, source_target_pairs={{0,16},{24,8},{1,17},{25,9},{2,18},{26,10},{3,19},{27,11},{4,20},{... | collective-permute-start | bytes 1327112 | tf_op jit(solution)/shard_map/cond/branch_1_fun/ppermute | solution.py:278
  150.3 23.5 %collective-permute-start.2 = (f32[288,384]{1,0:T(8,128)S(1)}, f32[288,384]{1,0:T(8,128)}, u32[]{:S(2)}, u32[]{:S(2)}) collective-permute-start(f32[288,384]{1,0:T(8,128)S(1)} %get-tuple-element.39), channel_id=1, source_target_pairs={{0,16},{8,24},{16,0},{24,8},{1,17},{9,25},{17,1},{25,9},{2,18},{10... | collective-permute-start | bytes 1327112 | tf_op jit(solution)/shard_map/cond/branch_1_fun/ppermute | solution.py:289
  154.1 28.1 %collective-permute-start.3 = (f32[288,384]{1,0:T(8,128)S(1)}, f32[288,384]{1,0:T(8,128)}, u32[]{:S(2)}, u32[]{:S(2)}) collective-permute-start(f32[288,384]{1,0:T(8,128)S(1)} %get-tuple-element.40), channel_id=1, source_target_pairs={{8,24},{16,0},{9,25},{17,1},{10,26},{18,2},{11,27},{19,3},{12,28},... | collective-permute-start | bytes 1327112 | tf_op jit(solution)/shard_map/cond/branch_1_fun/ppermute | solution.py:290
where the time goes:
time: 186 us
  blocking collectives  54.7 us (29%)
  Pallas kernels  45.9 us (25%)
  waiting for transfers between devices  38 us (20%)
  local copies, waits for them, and re-layouts  29.4 us (16%)
  other arithmetic  9.08 us (5%)
  starting transfers between devices  7.82 us (4%)
    pallas_call x3, Pallas kernels, call(): pl.pallas_call(body, out_shape=outs, in_specs=[pl.BlockSpec(memory_space=...  45.9 us
    all_to_all x1, blocking collectives, local(): here = lax.all_to_all(sent, 'slab', split_axis=0, concat_axis=0, tiled=True)  27.4 us
    all_to_all x1, blocking collectives, local(): back = lax.all_to_all(done, 'slab', split_axis=0, concat_axis=0, tiled=True)  27.4 us
    ppermute x1, waiting for transfers between devices, run(): lax.ppermute(both, 'grp', pairs(mask, None))  16.9 us
    ppermute x1, waiting for transfers between devices, run(): first = lax.ppermute(own[0], 'grp', pairs(mask, None))  12.6 us
    ppermute x1, waiting for transfers between devices, run(): lax.ppermute(second, 'grp', pairs(mask, False))  8.48 us
    cond x2, local copies, waits for them, and re-layouts  8.21 us
    pad x1, local copies, waits for them, and re-layouts, run(): cube = jnp.pad(cube, ((0, 0), (0, 0), (0, plan.padded - plan.period)))  4.94 us
  transfers between devices with their start and end apart: 4, of which 3 were waited for; matrix products, arithmetic and copies ran while one was open for 9% of the time, Pallas kernels for 0%

commit v1 on v0

v1 whole, which is shorter than its diff:
```python
import math

import jax
import jax.numpy as jnp
import ml_dtypes
import numpy as np
from jax import lax
from jax.experimental import pallas as pl
from jax.experimental.pallas import tpu as pltpu
from jax.sharding import PartitionSpec as P

LANE = 128


def halves(table):
    high = table.astype(np.float32).astype(ml_dtypes.bfloat16)
    low = (table - high.astype(np.float64)).astype(ml_dtypes.bfloat16)
    return np.stack([high, low])


class Plan:
    def __init__(self, planes, plane_cells, slabs, freqs):
        self.planes = planes
        self.grid = math.isqrt(plane_cells)
        self.slabs = slabs
        self.freqs = freqs
        self.period = 2 * self.grid
        self.group = math.lcm(self.grid, LANE)
        self.fold = self.group // self.grid
        self.chunks = self.grid // self.fold
        self.rows = planes * self.chunks
        self.groups = -(-planes // self.fold)
        self.lanes = self.groups * self.group
        self.wide = 2 * LANE
        self.starts = []
        for fold in range(self.fold):
            start = fold * self.grid // LANE * LANE
            self.starts.append(min(start, self.group - self.wide))
        self.spectrum = 2 * self.period
        self.sub = LANE // (2 * slabs)
        self.parts = freqs // self.sub
        self.block = 2 * self.sub
        self.padded = -(-self.period // self.wide) * self.wide

    def wave(self, left, right):
        angle = 2.0 * math.pi / self.period * (np.outer(left, right) % self.period)
        return np.cos(angle), np.sin(angle)

    def tables(self):
        grid, period, fold = self.grid, self.period, self.fold
        cells = np.arange(grid)
        waves = np.arange(period)
        cos, sin = self.wave(cells, waves)
        cosi, sini = cos.T / period, sin.T / period
        column = [
            (c, owner * self.freqs + part * self.sub + own)
            for part in range(self.parts)
            for owner in range(self.slabs)
            for c in range(2)
            for own in range(self.sub)
        ]
        side = np.array([c[0] for c in column])
        freq = np.array([c[1] for c in column])
        offsets = [j * grid - self.starts[j] for j in range(fold)]
        reach = max(offsets)
        self.slides = [reach - offset for offset in offsets]
        zf = np.zeros((2, reach + self.wide, self.spectrum))
        zi = np.zeros((fold, self.spectrum, 2, self.wide))
        yf = np.zeros((reach + self.wide, 2, self.padded))
        yi = np.zeros((fold, self.padded, 2, self.wide))
        y_order = np.array([fold * q + j for j in range(fold) for q in range(self.chunks)])
        at = slice(reach, reach + grid)
        zf[0, at] = np.where(side == 0, cos[:, freq], -sin[:, freq])
        zf[1, at] = np.where(side == 0, sin[:, freq], cos[:, freq])
        yf[at, 0, :period] = cos[y_order]
        yf[at, 1, :period] = sin[y_order]
        for j in range(fold):
            at = slice(j * grid - self.starts[j], (j + 1) * grid - self.starts[j])
            zi[j, :, 0, at] = np.where(side == 0, cosi[freq].T, -sini[freq].T).T
            zi[j, :, 1, at] = np.where(side == 0, sini[freq].T, cosi[freq].T).T
            yi[j, :period, 0, at] = cosi[:, y_order]
            yi[j, :period, 1, at] = sini[:, y_order]
        row = [
            (c, s * self.planes + x)
            for x in range(self.planes)
            for s in range(self.slabs)
            for c in range(2)
        ]
        side = np.array([r[0] for r in row])
        cell = np.array([r[1] for r in row])
        xf = np.concatenate(
            [
                np.where(side == 0, cos[cell].T, sin[cell].T),
                np.where(side == 0, -sin[cell].T, cos[cell].T),
            ]
        )
        xi = np.concatenate(
            [
                np.where(side == 0, cosi[:, cell], sini[:, cell]),
                np.where(side == 0, -sini[:, cell], cosi[:, cell]),
            ]
        ).T
        return {
            "zf": halves(zf),
            "zi": halves(zi.reshape(fold, self.spectrum, 2 * self.wide)),
            "yf": halves(yf.reshape(-1, 2 * self.padded)),
            "yi": halves(yi.reshape(fold, self.padded, 2 * self.wide)),
            "xf": halves(xf),
            "xi": halves(xi),
        }


def mm(left, right):
    return jnp.dot(left, right, preferred_element_type=jnp.float32)


def split(value):
    high = value.astype(jnp.bfloat16)
    low = (value - high.astype(jnp.float32)).astype(jnp.bfloat16)
    return high, low


def right_mul(value, high, low):
    vh, vl = value
    return mm(vh, high) + mm(vh, low) + mm(vl, high)


def left_mul(high, low, value):
    vh, vl = value
    return mm(high, vh) + mm(low, vh) + mm(high, vl)


def forward_z(plan, left, right, table_ref, turned):
    densities = [split(field * right) for field in left]
    chunks, grid, wide = plan.chunks, plan.grid, plan.wide
    used = plan.planes * grid
    if used < plan.lanes:
        turned[used:, :] = jnp.zeros((plan.lanes - used, plan.spectrum), jnp.float32)
    for j in range(plan.fold):
        at = slice(plan.starts[j], plan.starts[j] + wide)
        rows = slice(plan.slides[j], plan.slides[j] + wide)
        total = None
        for i in range(2):
            piece = tuple(d[:, at] for d in densities[i])
            term = right_mul(piece, table_ref[0, i, rows], table_ref[1, i, rows])
            total = term if total is None else total + term
        for x in range(plan.planes):
            first = x * grid + j * chunks
            turned[first : first + chunks, :] = total[x * chunks : (x + 1) * chunks]


def turn_out(plan, part, turned, out_ref):
    size = plan.slabs * plan.block
    for c in range(0, size, LANE):
        for r in range(0, plan.lanes, LANE):
            block = turned[r : r + LANE, part * size + c : part * size + c + LANE].T
            out_ref[part, c // plan.block : (c + LANE) // plan.block, :, r : r + LANE] = (
                block.reshape(LANE // plan.block, plan.block, LANE)
            )


def plane_work(plan, part, spread_ref, kernel_ref, yf_ref, yi_ref, xf_ref, xi_ref, out_ref, lines):
    slabs, sub, fold, wide = plan.slabs, plan.sub, plan.fold, plan.wide
    padded, size = plan.padded, plan.slabs * plan.block
    tiles = len(lines)
    for x in range(plan.planes):
        g, j = divmod(x, fold)
        start = g * plan.group + plan.starts[j]
        piece = split(spread_ref[part, :, :, start : start + wide].reshape(size, wide))
        rows = slice(plan.slides[j], plan.slides[j] + wide)
        both = right_mul(piece, yf_ref[0, rows], yf_ref[1, rows])
        both = both.reshape(slabs, 2, sub, 2 * padded)
        real = both[:, 0, :, :padded] + both[:, 1, :, padded:]
        imag = both[:, 1, :, :padded] - both[:, 0, :, padded:]
        mixed = jnp.stack([real, imag], axis=1).reshape(size, padded)
        for t in range(tiles):
            lines[t][x * size : (x + 1) * size, :] = mixed[:, t * LANE : (t + 1) * LANE]

    def one_plane(k, carry):
        rows = pl.ds(k, plan.planes * slabs * 2, stride=sub)
        field = jnp.concatenate([lines[t][rows, :] for t in range(tiles)], axis=1)
        spectra = left_mul(xf_ref[0], xf_ref[1], split(field))
        kernel = kernel_ref[part * sub + k]
        spectra = jnp.concatenate(
            [spectra[: plan.period] * kernel, spectra[plan.period :] * kernel], axis=0
        )
        back = left_mul(xi_ref[0], xi_ref[1], split(spectra))
        for t in range(tiles):
            lines[t][rows, :] = back[:, t * LANE : (t + 1) * LANE]
        return carry

    lax.fori_loop(0, sub, one_plane, 0)

    for g in range(plan.groups):
        total = [None] * (plan.group // LANE)
        for j in range(fold):
            x = g * fold + j
            if x >= plan.planes:
                break
            rows = slice(x * size, (x + 1) * size)
            field = jnp.concatenate([lines[t][rows, :] for t in range(tiles)], axis=1)
            both = right_mul(split(field), yi_ref[0, j], yi_ref[1, j])
            both = both.reshape(slabs, 2, sub, 2 * wide)
            real = both[:, 0, :, :wide] - both[:, 1, :, wide:]
            imag = both[:, 1, :, :wide] + both[:, 0, :, wide:]
            mixed = jnp.stack([real, imag], axis=1).reshape(size, wide)
            for t in range(wide // LANE):
                spot = plan.starts[j] // LANE + t
                term = mixed[:, t * LANE : (t + 1) * LANE]
                total[spot] = term if total[spot] is None else total[spot] + term
        for t, term in enumerate(total):
            if term is None:
                term = jnp.zeros((size, LANE), jnp.float32)
            first = g * plan.group + t * LANE
            out_ref[part, :, :, first : first + LANE] = term.reshape(slabs, plan.block, LANE)


def inverse_z(plan, part, spread_ref, table_ref, turned, field_ref):
    chunks, grid, wide = plan.chunks, plan.grid, plan.wide
    size = plan.slabs * plan.block
    for r in range(0, plan.lanes, LANE):
        for c in range(0, size, LANE):
            block = spread_ref[part, c // plan.block : (c + LANE) // plan.block, :, r : r + LANE]
            turned[r : r + LANE, c : c + LANE] = block.reshape(LANE, LANE).T
    total = [[None] * (plan.group // LANE) for _ in range(2)]
    own = slice(part * size, (part + 1) * size)
    for j in range(plan.fold):
        firsts = [x * grid + j * chunks for x in range(plan.planes)]
        rows = jnp.concatenate([turned[f : f + chunks, :size] for f in firsts], axis=0)
        both = right_mul(split(rows), table_ref[0, j, own], table_ref[1, j, own])
        for i in range(2):
            for t in range(wide // LANE):
                spot = plan.starts[j] // LANE + t
                first = i * wide + t * LANE
                term = both[:, first : first + LANE]
                known = total[i][spot]
                total[i][spot] = term if known is None else known + term
    for i in range(2):
        field = jnp.concatenate(total[i], axis=1)
        field_ref[i] = field if part == 0 else field_ref[i] + field


NAMES = ("zf", "yf", "xf", "cube", "xi", "yi", "zi")


def core(plan, *refs):
    flag_ref, *hbm = refs[:12]
    sent_ref, kept_ref = refs[12:14]
    vmem = refs[14:25]
    turned, going, coming, leaving, landing, field = refs[25:31]
    load_sem, send_sem, recv_sem = refs[31:34]
    lines = refs[34:]
    slabs, parts = plan.slabs, plan.parts
    loads = [
        pltpu.make_async_copy(source, dest, load_sem.at[n])
        for n, (source, dest) in enumerate(zip(hbm, vmem))
    ]
    for load in loads:
        load.start()
    me = lax.axis_index("slab")
    steps = sorted(range(1, slabs), key=lambda step: -step)
    barrier = pltpu.get_barrier_semaphore()
    for step in steps:
        pl.semaphore_signal(
            barrier, 1, device_id={"slab": me ^ step}, device_id_type=pl.DeviceIdType.MESH
        )
    pl.semaphore_wait(barrier, slabs - 1)

    def own_copy(way, part):
        source, dest = ((going, coming), (leaving, landing))[way]
        return pltpu.make_async_copy(
            source.at[part, me], dest.at[part, me], recv_sem.at[way, part, 0]
        )

    def remote(way, part, step, arriving):
        source, dest = ((going, coming), (leaving, landing))[way]
        peer = me ^ step
        return pltpu.make_async_remote_copy(
            src_ref=source.at[part, peer],
            dst_ref=dest.at[part, peer if arriving else me],
            send_sem=send_sem.at[way, part, step],
            recv_sem=recv_sem.at[way, part, step],
            device_id={"slab": peer},
            device_id_type=pl.DeviceIdType.MESH,
        )

    def send(way, part):
        for step in steps:
            remote(way, part, step, False).start()
        own_copy(way, part).start()

    def receive(way, part):
        own_copy(way, part).wait()
        for step in steps:
            remote(way, part, step, True).wait_recv()

    for load in loads[:5]:
        load.wait()
    own_first, own_second, first, second, zf, yf, xf, cube, xi, yi, zi = vmem
    flag = flag_ref[0] > 0
    left = [
        jnp.where(flag, own_first[...], first[...]),
        jnp.where(flag, own_second[...], second[...]),
    ]
    right = jnp.where(flag, first[...], own_second[...])
    forward_z(plan, left, right, zf, turned)
    for part in range(parts):
        turn_out(plan, part, turned, going)
        send(0, part)
    for load in loads[5:]:
        load.wait()
    for part in range(parts):
        receive(0, part)
        plane_work(plan, part, coming, cube, yf, yi, xf, xi, leaving, lines)
        send(1, part)
    for part in range(parts):
        receive(1, part)
        inverse_z(plan, part, landing, zi, turned, field)
    near = [field[0] * right, field[1] * right]
    far = field[0] * left[0] + field[1] * left[1]
    sent_ref[0] = jnp.where(flag, far, near[0])
    sent_ref[1] = near[1]
    kept_ref[0] = jnp.where(flag, near[0], jnp.zeros_like(far))
    kept_ref[1] = jnp.where(flag, near[1], far)
    for way in range(2):
        for part in range(parts):
            for step in steps:
                remote(way, part, step, False).wait_send()


def run_core(plan, flag, fields, tables, cube):
    f32 = jnp.float32
    operands = list(fields) + [cube if name == "cube" else tables[name] for name in NAMES]
    twin = jax.ShapeDtypeStruct((2, plan.rows, plan.group), f32)
    blocks = pltpu.VMEM((plan.parts, plan.slabs, plan.block, plan.lanes), f32)
    line = pltpu.VMEM((plan.planes * plan.slabs * plan.block, LANE), f32)
    return pl.pallas_call(
        lambda *refs: core(plan, *refs),
        out_shape=(twin, twin),
        in_specs=[pl.BlockSpec(memory_space=pltpu.SMEM)]
        + [pl.BlockSpec(memory_space=pl.ANY)] * len(operands),
        out_specs=(pl.BlockSpec(memory_space=pltpu.VMEM),) * 2,
        scratch_shapes=[pltpu.VMEM(op.shape, op.dtype) for op in operands]
        + [pltpu.VMEM((plan.lanes, plan.spectrum), f32)]
        + [blocks] * 4
        + [
            pltpu.VMEM(twin.shape, f32),
            pltpu.SemaphoreType.DMA((len(operands),)),
            pltpu.SemaphoreType.DMA((2, plan.parts, plan.slabs)),
            pltpu.SemaphoreType.DMA((2, plan.parts, plan.slabs)),
        ]
        + [line] * (plan.padded // LANE),
        compiler_params=pltpu.CompilerParams(
            collective_id=0, has_side_effects=True, vmem_limit_bytes=60 * 2**20
        ),
    )(flag, *operands)


def is_wide(group, mask):
    lower = jnp.minimum(group, group ^ mask)
    return (group == lower) == (lower % 2 == 0)


def local(orbitals, occupation, kernel_hat, pair_mask):
    orbit_count, planes, plane_cells = orbitals.shape
    assert orbit_count == 2
    slabs = lax.axis_size("slab")
    groups = lax.axis_size("grp")
    plan = Plan(planes, plane_cells, slabs, kernel_hat.shape[0])
    tables = {name: jnp.asarray(t) for name, t in plan.tables().items()}
    f32 = jnp.float32
    own_group = lax.axis_index("grp")
    partner_bits = pair_mask[0]
    wide_side = is_wide(own_group, partner_bits)
    scale = jnp.sqrt(0.25 * occupation.astype(f32))[:, None, None]
    own = [(orbitals[i] * scale[i]).reshape(plan.rows, plan.group) for i in range(2)]

    def pairs(mask, wanted):
        chosen = []
        for g in range(groups):
            lower = min(g, g ^ mask)
            wide = (g == lower) == (lower % 2 == 0)
            if wanted is None or wide == wanted:
                chosen.append((g, g ^ mask))
        return chosen

    def exchange(mask):
        def run(own, kernel_hat):
            first = lax.ppermute(own[0], "grp", pairs(mask, None))
            second = lax.ppermute(own[1], "grp", pairs(mask, True))
            cube = kernel_hat.reshape(-1, plan.period, plan.period)
            cube = jnp.swapaxes(cube, 1, 2)
            cube = jnp.pad(cube, ((0, 0), (0, 0), (0, plan.padded - plan.period)))
            return first, second, cube

        return run

    def give_back(mask):
        def run(sent):
            return (
                lax.ppermute(sent[0], "grp", pairs(mask, None)),
                lax.ppermute(sent[1], "grp", pairs(mask, False)),
            )

        return run

    masks = range(1, groups)
    index = partner_bits - 1
    first, second, cube = lax.switch(index, [exchange(m) for m in masks], own, kernel_hat)
    flag = wide_side.astype(jnp.int32).reshape(1)
    sent, kept = run_core(plan, flag, (own[0], own[1], first, second), tables, cube)
    back = lax.switch(index, [give_back(m) for m in masks], sent)
    total = [
        (kept[i] + back[i]).reshape(planes, plane_cells) * (-1.0 / scale[i]) for i in range(2)
    ]
    return jnp.stack(total)


def solution(mesh):
    return jax.shard_map(
        local,
        mesh=mesh,
        in_specs=(P("grp", "slab", None), P("grp"), P("slab", None), P()),
        out_specs=P("grp", "slab", None),
        check_vma=False,
    )
```

time: 186 us -> 129 us (0.69)
  blocking collectives: 54.7 us -> 0 us
  local copies, waits for them, and re-layouts: 29.4 us -> 19.9 us
  Pallas kernels: 45.9 us -> 53.7 us
  other arithmetic: 9.08 us -> 7.22 us
    all_to_all x2 -> x0, blocking collectives: 54.7 us -> none  [the longest x1 27.4 us: local(): here = lax.all_to_all(sent, 'slab', split_axis=0, concat_axis=0, tiled=True)]
    pallas_call x3 -> x1, Pallas kernels: 45.9 us -> 53.7 us  [run_core(): pl.pallas_call(lambda *refs: core(plan, *refs), out_shape=(twin, twin), i...]
    select_n x3 -> x0, other arithmetic: 5.07 us -> none  [the longest x1 2.15 us: local(): left = jnp.where(wide_side, own, jnp.stack([first, second]))]
    squeeze x3 -> x1, local copies, waits for them, and re-layouts: 5.07 us -> 0.06 us  [run(): sent[1]]
    mul x2, other arithmetic: 1.69 us -> 6.48 us  [the longest x1 5.24 us: local(): orbitals[i] * scale[i]]
    mul x2 -> x4, local copies, waits for them, and re-layouts: 2.9 us -> 0.28 us  [the longest x2 0.14 us: local(): (kept[i] + back[i]).reshape(planes, plane_cells) * (-1.0 / scale[i])]
    ppermute x1, waiting for transfers between devices: 12.6 us -> 10.1 us  [run(): first = lax.ppermute(own[0], 'grp', pairs(mask, None))]
    reshape x1 -> x0, local copies, waits for them, and re-layouts: 2.31 us -> none  [local(): own = (orbitals * scale).reshape(2, plan.rows, plan.group)]
  transfers between devices with their start and end apart: 4 -> 4, of which waited for: 3 -> 3; matrix products, arithmetic and copies ran while one was open for 9% -> 13% of each run, Pallas kernels for 0% -> 0%
where the time goes in v1:
time: 129 us; the launch traced here: 128 us
  Pallas kernels  53.7 us (42%)
  waiting for transfers between devices  37.7 us (29%)
  local copies, waits for them, and re-layouts  19.9 us (15%)
  starting transfers between devices  7.67 us (6%)
  other arithmetic  7.22 us (6%)
  between operations  2.06 us (2%)
    pallas_call x1, Pallas kernels, run_core(): pl.pallas_call(lambda *refs: core(plan, *refs), out_shape=(twin, twin), i...  53.7 us
    ppermute x1, waiting for transfers between devices, run(): lax.ppermute(sent[1], 'grp', pairs(mask, False))  19.3 us
    ppermute x1, waiting for transfers between devices, run(): first = lax.ppermute(own[0], 'grp', pairs(mask, None))  10.1 us
    ppermute x1, waiting for transfers between devices, run(): lax.ppermute(sent[0], 'grp', pairs(mask, None))  8.35 us
    cond x1, local copies, waits for them, and re-layouts  6.37 us
    ppermute x1, starting transfers between devices, run(): lax.ppermute(sent[1], 'grp', pairs(mask, False))  6.3 us
    reshape x1, local copies, waits for them, and re-layouts, run(): cube = kernel_hat.reshape(-1, plan.period, plan.period)  5.99 us
    mul x1, other arithmetic, local(): orbitals[i] * scale[i]  5.24 us
  transfers between devices with their start and end apart: 4, of which 3 were waited for; matrix products, arithmetic and copies ran while one was open for 13% of the time, Pallas kernels for 0%

profile of v1, /device:TPU:16, one launch (start us, length us, event | category | flops | bytes accessed | tf_op | source)
XLA Modules:
  0.0 128.3 jit_solution(10069777389792573916)
XLA Ops:
  0.7 0.7 multiply_sqrt_fusion
  1.3 0.7 fusion.2
  3.3 5.2 %multiply_reduce_fusion = (f32[12,9216]{1,0:T(8,128)S(1)}, f32[12,9216]{1,0:T(8,128)S(1)}) fusion(f32[2,12,9216]{2,0,1:T(2,128)} %param.16, f32[]{:T(128)} %bitcast.12, f32[]{:T(128)} %bitcast.11), kind=kLoop, calls=%fused_computation.11 | loop fusion | flops 221184 | bytes 1769480 | tf_op jit(solution)/shard_map/mul | solution.py:376
  8.6 0.1 mul.79.refs_2_
  8.6 0.1 mul.75.refs_1_
  8.7 28.8 %conditional.2 = (f32[288,384]{1,0:T(8,128)}, f32[288,384]{1,0:T(8,128)}, f32[24,192,256]{2,1,0:T(8,128)}) conditional(s32[]{:T(128)} %clamp.4, (f32[288,384]{1,0:T(8,128)S(1)}, f32[288,384]{1,0:T(8,128)S(1)}, f32[24,36864]{1,0:T(8,128)}) %tuple.29, (f32[288,384]{1,0:T(8,128)S(1)}, f32[288,384]{1,0:T(8,128)S(1)}, ...), branch_computations={%region_0.1_spmd, %region_1.2_spmd, %region_2.3_spmd} | conditional | bytes 25952364 | solution.py:409
  8.7 0.1 collective-permute-start.2
  8.8 1.3 %collective-permute-start.3 = (f32[288,384]{1,0:T(8,128)S(1)}, f32[288,384]{1,0:T(8,128)}, u32[]{:S(2)}, u32[]{:S(2)}) collective-permute-start(f32[288,384]{1,0:T(8,128)S(1)} %get-tuple-element.30), channel_id=1, source_target_pairs={{0,16},{24,8},{1,17},{25,9},{2,18},{26,10},{3,19},{27,11},{4,20},{... | collective-permute-start | bytes 1327112 | tf_op jit(solution)/shard_map/cond/branch_1_fun/ppermute | solution.py:390
  10.1 6.0 %reshape.56 = f32[24,192,192]{2,1,0:T(8,128)} reshape(f32[24,36864]{1,0:T(8,128)} %get-tuple-element.31) | data formatting | bytes 7077888 | tf_op jit(solution)/shard_map/cond/branch_1_fun/reshape | solution.py:391
  16.1 6.4 %copy.20 = f32[24,192,192]{2,1,0:T(8,128)} copy(f32[24,192,192]{1,2,0:T(8,128)} %bitcast.32) | data formatting | bytes 7077888 | tf_op jit(solution)/shard_map/cond
  22.5 4.9 %pad.8.clone = f32[24,192,256]{2,1,0:T(8,128)} pad(f32[24,192,192]{2,1,0:T(8,128)} %copy.20, f32[]{:T(128)} %constant.40.clone), padding=0_0x0_0x0_64 | pad | bytes 8257540 | tf_op jit(solution)/shard_map/cond/branch_1_fun/jit(_pad)/pad | solution.py:393
  27.4 10.1 %collective-permute-done.2 = f32[288,384]{1,0:T(8,128)} collective-permute-done((f32[288,384]{1,0:T(8,128)S(1)}, f32[288,384]{1,0:T(8,128)}, u32[]{:S(2)}, u32[]{:S(2)}) %collective-permute-start.2) | collective-permute-done | bytes 442400 | tf_op jit(solution)/shard_map/cond/branch_1_fun/ppermute | solution.py:389
  37.5 53.7 %shard_map.100 = (f32[2,288,384]{2,1,0:T(8,128)S(1)}, f32[2,288,384]{2,1,0:T(8,128)}) custom-call(s32[1]{0:T(128)} %bitcast.10.refs_0_, f32[288,384]{1,0:T(8,128)S(1)} %mul.75.refs_1_, f32[288,384]{1,0:T(8,128)S(1)} %mul.79.refs_2_, f32[288,384]{1,0:T(8,128)} %get-tuple-element.42.refs_3_, f32[288,384]{1,0:T(8,128)} %get-tuple-element.43.refs_4_, ...), custom_call_target="tpu_custom_call" | custom-call | tf_op jit(solution)/shard_map/pallas_call | solution.py:337
  91.2 34.0 %conditional.3 = (f32[288,384]{1,0:T(8,128)}, f32[288,384]{1,0:T(8,128)}) conditional(s32[]{:T(128)} %clamp.4, f32[2,288,384]{2,1,0:T(8,128)S(1)} %get-tuple-element.46, f32[2,288,384]{2,1,0:T(8,128)S(1)} %get-tuple-element.46, f32[2,288,384]{2,1,0:T(8,128)S(1)} %get-tuple-element.46), branch_computations={%region_3.4_spmd, %region_4.5_spmd, %region_5.6_spmd} | conditional | bytes 5308512 | solution.py:412
  91.2 0.1 slice_bitcast_fusion.2
  91.3 6.3 %collective-permute-start.9 = (f32[288,384]{1,0:T(8,128)S(1)}, f32[288,384]{1,0:T(8,128)}, u32[]{:S(2)}, u32[]{:S(2)}) collective-permute-start(f32[288,384]{1,0:T(8,128)S(1)} %get-tuple-element.54), channel_id=1, source_target_pairs={{8,24},{16,0},{9,25},{17,1},{10,26},{18,2},{11,27},{19,3},{12,28},... | collective-permute-start | bytes 1327112 | tf_op jit(solution)/shard_map/cond/branch_1_fun/ppermute | solution.py:402
  97.6 0.0 collective-permute-start.8
  97.6 19.3 %collective-permute-done.9 = f32[288,384]{1,0:T(8,128)} collective-permute-done((f32[288,384]{1,0:T(8,128)S(1)}, f32[288,384]{1,0:T(8,128)}, u32[]{:S(2)}, u32[]{:S(2)}) %collective-permute-start.9) | collective-permute-done | bytes 442400 | tf_op jit(solution)/shard_map/cond/branch_1_fun/ppermute | solution.py:402
  116.9 8.3 %collective-permute-done.8 = f32[288,384]{1,0:T(8,128)} collective-permute-done((f32[288,384]{1,0:T(8,128)S(1)}, f32[288,384]{1,0:T(8,128)}, u32[]{:S(2)}, u32[]{:S(2)}) %collective-permute-start.8) | collective-permute-done | bytes 442400 | tf_op jit(solution)/shard_map/cond/branch_1_fun/ppermute | solution.py:401
  125.2 1.2 fusion.1
  126.4 0.1 mul.83
  126.5 0.1 mul.87
  126.6 0.1 pad_maximum_fusion
  126.7 1.6 %copy.15 = f32[2,12,9216]{2,0,1:T(2,128)} copy(f32[2,12,9216]{2,1,0:T(8,128)S(1)} %pad_maximum_fusion) | data formatting | bytes 1769472 | tf_op jit(solution)/shard_map/stack | solution.py:416
  (3 shorter events, 0.0 us)
Async XLA Ops:
  8.7 28.7 %collective-permute-start.2 = (f32[288,384]{1,0:T(8,128)S(1)}, f32[288,384]{1,0:T(8,128)}, u32[]{:S(2)}, u32[]{:S(2)}) collective-permute-start(f32[288,384]{1,0:T(8,128)S(1)} %get-tuple-element.29), channel_id=1, source_target_pairs={{0,16},{8,24},{16,0},{24,8},{1,17},{9,25},{17,1},{25,9},{2,18},{10... | collective-permute-start | bytes 1327112 | tf_op jit(solution)/shard_map/cond/branch_1_fun/ppermute | solution.py:389
  8.8 28.7 %collective-permute-start.3 = (f32[288,384]{1,0:T(8,128)S(1)}, f32[288,384]{1,0:T(8,128)}, u32[]{:S(2)}, u32[]{:S(2)}) collective-permute-start(f32[288,384]{1,0:T(8,128)S(1)} %get-tuple-element.30), channel_id=1, source_target_pairs={{0,16},{24,8},{1,17},{25,9},{2,18},{26,10},{3,19},{27,11},{4,20},{... | collective-permute-start | bytes 1327112 | tf_op jit(solution)/shard_map/cond/branch_1_fun/ppermute | solution.py:390
  91.2 34.0 %copy-start = (f32[2,288,384]{2,1,0:T(8,128)S(1)}, f32[2,288,384]{2,1,0:T(8,128)}, u32[]{:S(2)}) copy-start(f32[2,288,384]{2,1,0:T(8,128)} %get-tuple-element.45) | copy-start | bytes 2654212
  91.3 25.6 %collective-permute-start.9 = (f32[288,384]{1,0:T(8,128)S(1)}, f32[288,384]{1,0:T(8,128)}, u32[]{:S(2)}, u32[]{:S(2)}) collective-permute-start(f32[288,384]{1,0:T(8,128)S(1)} %get-tuple-element.54), channel_id=1, source_target_pairs={{8,24},{16,0},{9,25},{17,1},{10,26},{18,2},{11,27},{19,3},{12,28},... | collective-permute-start | bytes 1327112 | tf_op jit(solution)/shard_map/cond/branch_1_fun/ppermute | solution.py:402
  97.6 27.6 %collective-permute-start.8 = (f32[288,384]{1,0:T(8,128)S(1)}, f32[288,384]{1,0:T(8,128)}, u32[]{:S(2)}, u32[]{:S(2)}) collective-permute-start(f32[288,384]{1,0:T(8,128)S(1)} %get-tuple-element.55), channel_id=1, source_target_pairs={{0,16},{8,24},{16,0},{24,8},{1,17},{9,25},{17,1},{25,9},{2,18},{10... | collective-permute-start | bytes 1327112 | tf_op jit(solution)/shard_map/cond/branch_1_fun/ppermute | solution.py:401
